TPU v7x, 256 devices: a whole 4x4x8 slice. The times are simulated.
256 devices in a mesh: rep: 16 (over y, z_hi, core), tp: 16 (over x, z_lo).
Axes of the slice: x: 4, y: 4, z: 8 (z_hi: 2, z_lo: 4; z = z_hi * 4 + z_lo), core: 2. Of those that a mesh axis runs over, the one named last changes fastest.
Arguments:
- activations: bfloat16 [16, 2048, 4096], P('rep', 'tp'), may hold values from -6 to 6
- cotangent: bfloat16 [16, 2048, 8192], P('rep', None, 'tp'), may hold values from -0.13183594 to 0.13183594
- drift: bfloat16 [16, 4096, 8192], P('rep', None, 'tp'), may hold values from -8 to 8
- outer_weights: float32 [4096, 8192], P(('rep', 'tp')), may hold values from -6 to 6
- momentum: float32 [4096, 8192], P(('rep', 'tp')), may hold values from -6 to 6
Outputs:
- weights: bfloat16 [4096, 8192], P(None, 'tp')
- new_outer: float32 [4096, 8192], P(('rep', 'tp'))
- new_momentum: float32 [4096, 8192], P(('rep', 'tp'))
All inputs are finite; a program needn't handle non-finite values.
Results may differ from a plain program's by a relative error of at most 0.0085.
Values may be sent and summed in bfloat16 or wider, within the bound.
A program may use at most 128 MiB of HBM per device.

v0:
```python
import jax
import jax.numpy as jnp
from jax import lax
from jax.sharding import Mesh
from jax.sharding import PartitionSpec as P

TP = ("tp_0", "tp_1")
REP_TP = ("rep", "tp_0", "tp_1")


outer_rate = 0.7
nesterov = 0.9


def gathered_by_axis(shard, axes, dim):
    if not axes:
        return shard
    nearer = lax.all_gather(shard, axes[-1], axis=dim, tiled=True)
    return gathered_by_axis(nearer, axes[:-1], dim)


def on_device(activations, cotangent, drift, outer_weights, momentum):
    replicas = lax.axis_size("rep")
    cot_rows = cotangent[0]
    grad = jnp.einsum(
        "td,tf->df",
        gathered_by_axis(activations, TP, 1)[0],
        cot_rows,
        preferred_element_type=jnp.float32,
    )
    delta = lax.optimization_barrier((drift[0].astype(jnp.float32) + grad).astype(jnp.bfloat16))
    summed = lax.psum_scatter(
        delta.astype(jnp.float32).astype(jnp.bfloat16), "rep", scatter_dimension=0, tiled=True
    ).astype(jnp.float32)
    summed = lax.all_to_all(
        summed.astype(jnp.bfloat16), TP, split_axis=0, concat_axis=1, tiled=True
    ).astype(summed.dtype)
    average = summed / replicas
    new_momentum = nesterov * momentum + average
    new_outer = outer_weights - outer_rate * (average + nesterov * new_momentum)
    rounded = new_outer.astype(jnp.bfloat16)
    part = lax.all_to_all(rounded, TP, split_axis=1, concat_axis=0, tiled=True)
    weights = lax.all_gather(part, "rep", axis=0, tiled=True)
    return (weights, new_outer, new_momentum)


def solution(mesh):
    split = Mesh(mesh.devices.reshape(mesh.shape["rep"], 4, 4), ("rep", "tp_0", "tp_1"))
    in_specs = (
        P("rep", TP, None),
        P("rep", None, TP),
        P("rep", None, TP),
        P(REP_TP, None),
        P(REP_TP, None),
    )
    out_specs = (P(None, TP), P(REP_TP, None), P(REP_TP, None))
    return jax.shard_map(
        on_device, mesh=split, in_specs=in_specs, out_specs=out_specs, check_vma=False
    )
```

profile of v0, /device:TPU:1, one launch (start us, length us, event | category | flops | bytes accessed | tf_op | source)
XLA Modules:
  0.0 488.0 jit_solution(10202288569812770123)
XLA Ops:
  7.2 0.0 copy-start
  7.2 0.0 all-gather.4.cloned.1.call-start
  7.2 0.7 all-gather.4.cloned.1.call-update
  7.9 0.0 all-gather.6.cloned.1.call-start
  8.0 89.4 %all-gather.4.cloned.1.call-done = bf16[1,512,4096]{2,1,0:T(8,128)(2,1)} async-done(((bf16[1,128,4096]{2,1,0:T(8,128)(2,1)}), bf16[1,512,4096]{2,1,0:T(8,128)(2,1)}) %all-gather.4.cloned.1.call-update) | async-done | bytes 4194320 | tf_op jit(solution)/shard_map/all_gather | solution.py:18
  97.4 0.0 all-gather.6.cloned.1.call-update
  97.4 0.0 reduce-scatter.2.cloned.1.call-start
  97.4 158.5 %all-gather.6.cloned.1.call-done = bf16[1,2048,4096]{2,1,0:T(8,128)(2,1)} async-done(((bf16[1,512,4096]{2,1,0:T(8,128)(2,1)}), bf16[1,2048,4096]{2,1,0:T(8,128)(2,1)}) %all-gather.6.cloned.1.call-update) | async-done | bytes 16777232 | tf_op jit(solution)/shard_map/all_gather | solution.py:18
  255.9 0.0 copy-done
  255.9 14.4 %fusion.2 = bf16[4096,512]{1,0:T(8,128)(2,1)} fusion(bf16[1,2048,4096]{2,1,0:T(8,128)(2,1)} %all-gather.6.cloned.1.call-done, bf16[1,4096,512]{2,1,0:T(8,128)(2,1)} %param.7, bf16[1,2048,512]{2,1,0:T(8,128)(2,1)S(1)} %copy-done), kind=kOutput, calls=%fused_computation.3 | convolution fusion | flops 8596226048 | bytes 27262976 | tf_op jit(solution)/shard_map/td,tf->df/dot_general | solution.py:25
  270.4 0.0 copy-start.1
  270.4 0.0 copy-start.2
  270.4 0.0 reduce-scatter.2.cloned.1.call-update
  270.4 0.0 all-gather.8.cloned.1.call-start
  270.4 103.5 %reduce-scatter.2.cloned.1.call-done = bf16[256,512]{1,0:T(8,128)(2,1)} async-done(((bf16[4096,512]{1,0:T(8,128)(2,1)}), bf16[256,512]{1,0:T(8,128)(2,1)}) %reduce-scatter.2.cloned.1.call-update) | async-done | bytes 262160 | tf_op jit(solution)/shard_map/reduce_scatter | solution.py:32
  374.0 12.9 %all_to_all.32 = bf16[16,16,512]{2,1,0:T(8,128)(2,1)S(1)} all-to-all(bf16[16,16,512]{2,1,0:T(8,128)(2,1)} %bitcast.27), channel_id=1, replica_groups=mesh['rep'=16,'tp_0'=4,'tp_1'=4] {'tp_0','tp_1'}, dimensions={0} | all-to-all | bytes 524288 | tf_op jit(solution)/shard_map/all_to_all | solution.py:35
  386.8 0.1 multiply_bitcast_fusion
  387.0 0.0 copy-done.1
  387.0 0.0 copy-done.2
  387.0 1.1 fusion.6
  388.1 11.3 %all_to_all.33 = bf16[16,16,512]{2,0,1:T(8,128)(2,1)} all-to-all(bf16[16,16,512]{2,0,1:T(8,128)(2,1)S(1)} %bitcast.25), channel_id=1, replica_groups=mesh['rep'=16,'tp_0'=4,'tp_1'=4] {'tp_0','tp_1'}, dimensions={1} | all-to-all | bytes 524288 | tf_op jit(solution)/shard_map/all_to_all | solution.py:42
  399.4 0.0 all-gather.8.cloned.1.call-update
  399.4 77.6 %all-gather.8.cloned.1.call-done = bf16[4096,512]{1,0:T(8,128)(2,1)} async-done(((bf16[256,512]{1,0:T(8,128)(2,1)}), bf16[4096,512]{1,0:T(8,128)(2,1)}) %all-gather.8.cloned.1.call-update) | async-done | bytes 4194320 | tf_op jit(solution)/shard_map/all_gather | solution.py:43
  477.0 4.5 copy.18
  (2 shorter events, 0.1 us)
Async XLA Ops:
  7.2 248.8 %copy-start = (bf16[1,2048,512]{2,1,0:T(8,128)(2,1)S(1)}, bf16[1,2048,512]{2,1,0:T(8,128)(2,1)}, u32[]{:S(2)}) copy-start(bf16[1,2048,512]{2,1,0:T(8,128)(2,1)} %param.6) | copy-start | bytes 6291460
  7.2 90.2 %all-gather.4.cloned.1.call-start = ((), (), s32[]{:S(2)}) async-start(), calls=%async_computation.3 | async-start | bytes 5242880 | tf_op jit(solution)/shard_map/all_gather | solution.py:18
  7.9 248.0 %all-gather.6.cloned.1.call-start = ((), (), s32[]{:S(2)}) async-start(), calls=%async_computation.4 | async-start | bytes 20971520 | tf_op jit(solution)/shard_map/all_gather | solution.py:18
  97.4 276.6 %reduce-scatter.2.cloned.1.call-start = ((), (), s32[]{:S(2)}) async-start(), calls=%async_computation.5 | async-start | bytes 4456448 | tf_op jit(solution)/shard_map/reduce_scatter | solution.py:32
  270.4 116.6 %copy-start.1 = (f32[16,8192]{1,0:T(8,128)S(1)}, f32[16,8192]{1,0:T(8,128)}, u32[]{:S(2)}) copy-start(f32[16,8192]{1,0:T(8,128)} %param.8) | copy-start | bytes 1572868
  270.4 116.6 %copy-start.2 = (f32[16,8192]{1,0:T(8,128)S(1)}, f32[16,8192]{1,0:T(8,128)}, u32[]{:S(2)}) copy-start(f32[16,8192]{1,0:T(8,128)} %param.9) | copy-start | bytes 1572868
  270.4 206.6 %all-gather.8.cloned.1.call-start = ((), (), s32[]{:S(2)}) async-start(), calls=%async_computation.6 | async-start | bytes 4456448 | tf_op jit(solution)/shard_map/all_gather | solution.py:43
Sparse Core Ops, SparseCore 0:
  9.8 87.5 all-gather.3
  99.2 156.7 all-gather.5
  270.5 103.4 reduce-scatter.1
  399.5 77.4 all-gather.7
where the time goes:
time: 488 us
  waiting for transfers between devices  430 us (88%)
  blocking collectives  24.2 us (5%)
  matrix products  14.4 us (3%)
  between operations  13.8 us (3%)
    all_gather x2, waiting for transfers between devices, gathered_by_axis(): nearer = lax.all_gather(shard, axes[-1], axis=dim, tiled=True)  248 us
    reduce_scatter x1, waiting for transfers between devices, on_device(): lax.psum_scatter(delta.astype(jnp.float32).astype(jnp.bfloat16), 'rep', s...  104 us
    all_gather x1, waiting for transfers between devices, on_device(): weights = lax.all_gather(part, 'rep', axis=0, tiled=True)  77.6 us
    dot_general x1, matrix products, on_device(): jnp.einsum('td,tf->df', gathered_by_axis(activations, TP, 1)[0], cot_rows...  14.4 us
    all_to_all x1, blocking collectives, on_device(): lax.all_to_all(summed.astype(jnp.bfloat16), TP, split_axis=0, concat_axis...  12.9 us
    all_to_all x1, blocking collectives, on_device(): part = lax.all_to_all(rounded, TP, split_axis=1, concat_axis=0, tiled=True)  11.3 us
  transfers between devices with their start and end apart: 4, of which 4 were waited for; matrix products, arithmetic and copies ran while one was open for 0% of the time, Pallas kernels for 0%

commit v1 on v0

v1 whole, which is shorter than its diff:
```python
import functools

import jax
import jax.numpy as jnp
from jax import lax
from jax.experimental import pallas as pl
from jax.experimental.pallas import tpu as pltpu
from jax.sharding import PartitionSpec as P

outer_rate = 0.7
nesterov = 0.9

F32 = jnp.float32
BF16 = jnp.bfloat16
MESH = pl.DeviceIdType.MESH
N_SEND = 160
N_RECV = 160
N_LOCAL = 32


def kernel(at, cot, drift, outer, mom, wout, no_out, nm_out,
           abuf, cbuf, dbuf, pbuf, y1, y2, rbuf, zr, fbuf, xr, wsend, w1, obuf, mbuf,
           ss, rs, ls):
    rep = lax.axis_index("rep")
    tp = lax.axis_index("tp")
    y = rep // 4
    zhi = (rep // 2) % 2
    c = rep % 2
    x = tp // 4
    zlo = tp % 4
    z = zhi * 4 + zlo
    oc = 1 - c

    def dev(yy, zz, cc, xx):
        return ((yy % 4) * 4 + ((zz % 8) // 4) * 2 + cc, (xx % 4) * 4 + (zz % 4))

    counts = {"s": 0, "r": 0, "l": 0}
    sends = []

    def take(kind, n=1):
        base = counts[kind]
        counts[kind] += n
        return base

    def send(src, dst, to, rsem):
        copy = pltpu.make_async_remote_copy(
            src_ref=src, dst_ref=dst, send_sem=ss.at[take("s")], recv_sem=rs.at[rsem],
            device_id=to, device_id_type=MESH)
        copy.start()
        sends.append(copy)

    def arrive(ref, rsem):
        pltpu.make_async_copy(ref, ref, rs.at[rsem]).wait()

    def local(src, dst):
        copy = pltpu.make_async_copy(src, dst, ls.at[take("l")])
        copy.start()
        return copy

    partner = dev(y, z, oc, x)
    up, down = dev(y + 1, z, c, x), dev(y - 1, z, c, x)
    zup, zdown = dev(y, z + 1, c, x), dev(y, z - 1, c, x)

    greeted = [partner, up, down]
    greeted += [dev(y, z, cc, x + d) for d in (1, 3) for cc in (0, 1)]
    greeted += [dev(y, z, c, x + 2)]
    greeted += [dev(y, z + k, c, x) for k in range(1, 8)]
    barrier = pltpu.get_barrier_semaphore()
    for other in greeted:
        pl.semaphore_signal(barrier, inc=1, device_id=other, device_id_type=MESH)

    def lanes(group, xx):
        return pl.ds(pl.multiple_of((group * 4 + xx % 4) * 128, 128), 128)

    a_own = [local(at.at[:, c, r], abuf.at[r, :, :, lanes(c, x)]) for r in range(2)]
    c_own = local(cot.at[:, zlo], cbuf.at[zlo, c])
    d_own = [local(drift.at[:, c, r], dbuf.at[0, r]) for r in range(2)]
    o_own = local(outer, obuf)
    m_own = local(mom, mbuf)
    pl.semaphore_wait(barrier, len(greeted))

    a_part = take("r", 2)
    a_minus = take("r", 4)
    a_plus = take("r", 4)
    a_far = take("r", 4)
    c_part = take("r", 4)
    c_peer = take("r", 4)
    d_part = take("r", 2)

    def send_a(r):
        dst = abuf.at[r, :, :, lanes(c, x)]
        send(at.at[:, c, r], dst, dev(y, z, c, x + 1), a_minus + 2 * r + c)
        send(at.at[:, c, r], dst, dev(y, z, c, x - 1), a_plus + 2 * r + c)
        send(at.at[:, oc, r], dst, dev(y, z, oc, x + 1), a_minus + 2 * r + c)
        send(at.at[:, oc, r], dst, dev(y, z, oc, x - 1), a_plus + 2 * r + c)
        send(at.at[:, oc, r], dst, partner, a_part + r)

    def forward_a(r):
        for group in range(2):
            arrive(abuf.at[r, :, :, lanes(group, x - 1)], a_minus + 2 * r + group)
        src = abuf.at[r, :, :, lanes(0, x - 1)]
        send(src, src, dev(y, z, c, x + 1), a_far + 2 * r)
        for group in range(2):
            arrive(abuf.at[r, :, :, lanes(group, x + 1)], a_plus + 2 * r + group)
        src = abuf.at[r, :, :, lanes(1, x + 1)]
        send(src, src, dev(y, z, c, x - 1), a_far + 2 * r + 1)

    def finish_a(r):
        a_own[r].wait()
        arrive(abuf.at[r, :, :, lanes(oc, x)], a_part + r)
        for group in range(2):
            arrive(abuf.at[r, :, :, lanes(group, x + 2)], a_far + 2 * r + group)

    offsets = (0, 1, 3, 2)

    send_a(0)
    send(cot.at[:, zlo], cbuf.at[zlo, c], partner, c_part)
    send(drift.at[:, oc, 0], dbuf.at[1, 0], partner, d_part)
    for s in (1, 2, 3):
        to = (zlo - offsets[s]) % 4
        send(cot.at[:, to], cbuf.at[zlo, c], dev(y, zhi * 4 + to, c, x), c_peer + s)
    send_a(1)
    send(drift.at[:, oc, 1], dbuf.at[1, 1], partner, d_part + 1)

    def ready_c(s):
        q = (zlo + offsets[s]) % 4
        if s == 0:
            c_own.wait()
        else:
            arrive(cbuf.at[q, c], c_peer + s)
            send(cbuf.at[q, c], cbuf.at[q, c], partner, c_part + s)
        arrive(cbuf.at[q, oc], c_part + s)

    y_first = take("r", 16)
    y_plain = take("r", 16)
    y_sum = take("r", 16)

    def compute(r, s):
        unit = r * 4 + s
        q = (zlo + offsets[s]) % 4
        if r == 0:
            ready_c(s)
        if s == 0:
            d_own[r].wait()
            arrive(dbuf.at[1, r], d_part + r)

        def piece(j, carry):
            yy = (y + j) % 4
            lhs = abuf[r, pl.ds(yy * 2, 2)].reshape(256, 1024)
            rhs = cbuf[q].reshape(1024, 512)
            total = jnp.dot(lhs, rhs, preferred_element_type=F32)
            if s == 0:
                total = total + dbuf[0, r, pl.ds(yy * 2, 2)].reshape(256, 512).astype(F32)
                total = total + dbuf[1, r, pl.ds(yy * 2, 2)].reshape(256, 512).astype(F32)
            pbuf[r, s, j] = total.astype(BF16)
            return carry

        lax.fori_loop(0, 4, piece, 0)
        low, high = pl.ds(0, 128), pl.ds(128, 128)
        send(pbuf.at[r, s, 2, low], y1.at[0, r, s], up, y_first + unit)
        send(pbuf.at[r, s, 2, high], y1.at[1, r, s], down, y_first + 8 + unit)
        send(pbuf.at[r, s, 1, high], y2.at[0, r, s, high], up, y_plain + unit)
        send(pbuf.at[r, s, 3, low], y2.at[1, r, s, low], down, y_plain + 8 + unit)

    def relay_y(r, s):
        unit = r * 4 + s
        low, high = pl.ds(0, 128), pl.ds(128, 128)
        arrive(y1.at[0, r, s], y_first + unit)
        pbuf[r, s, 1, low] = (pbuf[r, s, 1, low].astype(F32) + y1[0, r, s].astype(F32)).astype(BF16)
        send(pbuf.at[r, s, 1, low], y2.at[0, r, s, low], up, y_sum + unit)
        arrive(y1.at[1, r, s], y_first + 8 + unit)
        pbuf[r, s, 3, high] = (pbuf[r, s, 3, high].astype(F32) + y1[1, r, s].astype(F32)).astype(BF16)
        send(pbuf.at[r, s, 3, high], y2.at[1, r, s, high], down, y_sum + 8 + unit)

    def finish_y(r, s):
        unit = r * 4 + s
        q = (zlo + offsets[s]) % 4
        low, high = pl.ds(0, 128), pl.ds(128, 128)
        arrive(y2.at[0, r, s, high], y_plain + unit)
        arrive(y2.at[1, r, s, low], y_plain + 8 + unit)
        arrive(y2.at[0, r, s, low], y_sum + unit)
        arrive(y2.at[1, r, s, high], y_sum + 8 + unit)
        for hi in range(2):
            for px in range(2):
                for pz in range(4):
                    rows = pl.ds(hi * 128 + px * 64 + pz * 16, 16)
                    total = (pbuf[r, s, 0, rows].astype(F32) + y2[0, r, s, rows].astype(F32)
                             + y2[1, r, s, rows].astype(F32))
                    rbuf[r, hi * 4 + pz, q, px] = total.astype(BF16)

    z_up = take("r", 8)
    z_down = take("r", 8)

    def ring_z(r, step):
        lo, hi = pl.ds(0, 2), pl.ds(2, 2)
        if step == 0:
            far = (z + 4) % 8
            send(rbuf.at[r, far, lo], zr.at[0, r, 0, lo], zup, z_up + 4 * r)
            send(rbuf.at[r, far, hi], zr.at[1, r, 0, hi], zdown, z_down + 4 * r)
            return
        last = step == 4
        for way, (base, to) in enumerate(((z_up, zup), (z_down, zdown))):
            part = (lo, hi)[way] if step == 1 else pl.ds(0, 4)
            arrive(zr.at[way, r, step - 1, part], base + 4 * r + step - 1)
            if not last:
                target = (z + (4 - step)) % 8 if way == 0 else (z + 4 + step) % 8
                rbuf[r, target, part] = (rbuf[r, target, part].astype(F32)
                                         + zr[way, r, step - 1, part].astype(F32)).astype(BF16)
                send(rbuf.at[r, target], zr.at[way, r, step], to, base + 4 * r + step)
        if last:
            for q in range(4):
                for px in range(2):
                    total = (rbuf[r, z, q, px].astype(F32) + zr[0, r, 3, q, px].astype(F32)
                             + zr[1, r, 3, q, px].astype(F32))
                    fbuf[2 * r + px, q] = total.astype(BF16)

    forward_a(0)
    finish_a(0)
    compute(0, 0)
    compute(0, 1)
    relay_y(0, 0)
    compute(0, 2)
    relay_y(0, 1)
    forward_a(1)
    finish_y(0, 0)
    compute(0, 3)
    relay_y(0, 2)
    finish_y(0, 1)
    finish_a(1)
    compute(1, 0)
    relay_y(0, 3)
    finish_y(0, 2)
    compute(1, 1)
    relay_y(1, 0)
    finish_y(0, 3)
    ring_z(0, 0)
    compute(1, 2)
    relay_y(1, 1)
    finish_y(1, 0)
    ring_z(0, 1)
    compute(1, 3)
    relay_y(1, 2)
    finish_y(1, 1)
    ring_z(0, 2)
    relay_y(1, 3)
    finish_y(1, 2)
    ring_z(0, 3)
    finish_y(1, 3)
    ring_z(1, 0)
    ring_z(0, 4)
    for step in range(1, 5):
        ring_z(1, step)

    x_in = take("r", 4)
    for d in (1, 3, 2):
        xx = (x + d) % 4
        send(fbuf.at[xx], xr.at[x], dev(y, z, c, xx), x_in + d)
    xr[x] = fbuf[x]
    o_own.wait()
    m_own.wait()
    for d in (1, 3, 2):
        arrive(xr.at[(x - d) % 4], x_in + d)

    for xx in range(4):
        for q in range(4):
            cols = pl.ds((xx * 4 + q) * 512, 512)
            average = xr[xx, q].astype(F32) / 16
            momentum = nesterov * mbuf[:, cols] + average
            weights = obuf[:, cols] - outer_rate * (average + nesterov * momentum)
            mbuf[:, cols] = momentum
            obuf[:, cols] = weights
            wsend[xx, q] = weights.astype(BF16)

    r_one = take("r", 4)
    for d in (1, 3, 2):
        xx = (x + d) % 4
        send(wsend.at[xx], w1.at[x], dev(y, z, c, xx), r_one + d)
    w1[x] = wsend[x]
    o_done = local(obuf, no_out)
    m_done = local(mbuf, nm_out)
    for d in (1, 3, 2):
        arrive(w1.at[(x - d) % 4], r_one + d)

    r_two = take("r", 8)
    own = wout.at[rep, :, zlo]
    for k in (4, 3, 5, 2, 6, 1, 7):
        zz = (z + k) % 8
        send(w1.at[:, zz % 4], own, dev(y, zz, c, x), r_two + k)
    own_done = local(w1.at[:, zlo], own)

    def block(yy, half, cc):
        return wout.at[(yy % 4) * 4 + 2 * half + cc]

    r_up = take("r", 2)
    r_down = take("r", 2)
    r_far = take("r", 2)
    r_part = take("r", 8)
    own_done.wait()
    for k in (1, 7, 2, 6, 3, 5, 4):
        zz = (z - k) % 8
        arrive(wout.at[y * 4 + (zz // 4) * 2 + c, :, zz % 4], r_two + k)
    for half in range(2):
        src = block(y, half, c)
        send(src, src, up, r_down + half)
        send(src, src, down, r_up + half)
    for half in range(2):
        src = block(y, half, c)
        send(src, src, partner, r_part + half)
    for half in range(2):
        src = block(y - 1, half, c)
        arrive(src, r_down + half)
        if half == 0:
            send(src, src, up, r_far)
        send(src, src, partner, r_part + 2 + half)
        half = 1 - half
        src = block(y + 1, half, c)
        arrive(src, r_up + half)
        if half == 1:
            send(src, src, down, r_far + 1)
        send(src, src, partner, r_part + 4 + half)
    for half in range(2):
        src = block(y + 2, half, c)
        arrive(src, r_far + half)
        send(src, src, partner, r_part + 6 + half)
    for half in range(2):
        arrive(block(y, half, oc), r_part + half)
        arrive(block(y - 1, half, oc), r_part + 2 + half)
        arrive(block(y + 1, half, oc), r_part + 4 + half)
        arrive(block(y + 2, half, oc), r_part + 6 + half)
    o_done.wait()
    m_done.wait()
    for copy in sends:
        copy.wait_send()


def on_device(activations, cotangent, drift, outer_weights, momentum):
    at = activations[0].T.reshape(8, 2, 2, 128, 128)
    cot = cotangent[0].reshape(4, 4, 128, 512)
    dr = drift[0].reshape(8, 2, 2, 128, 512)
    any_spec = pl.BlockSpec(memory_space=pl.ANY)
    weights, new_outer, new_momentum = pl.pallas_call(
        kernel,
        out_shape=(
            jax.ShapeDtypeStruct((16, 4, 4, 16, 512), BF16),
            jax.ShapeDtypeStruct((16, 8192), F32),
            jax.ShapeDtypeStruct((16, 8192), F32),
        ),
        in_specs=[any_spec] * 5,
        out_specs=[any_spec] * 3,
        scratch_shapes=[
            pltpu.VMEM((2, 8, 128, 1024), BF16),
            pltpu.VMEM((4, 2, 4, 128, 512), BF16),
            pltpu.VMEM((2, 2, 8, 128, 512), BF16),
            pltpu.VMEM((2, 4, 4, 256, 512), BF16),
            pltpu.VMEM((2, 2, 4, 128, 512), BF16),
            pltpu.VMEM((2, 2, 4, 256, 512), BF16),
            pltpu.VMEM((2, 8, 4, 2, 16, 512), BF16),
            pltpu.VMEM((2, 2, 4, 4, 2, 16, 512), BF16),
            pltpu.VMEM((4, 4, 16, 512), BF16),
            pltpu.VMEM((4, 4, 16, 512), BF16),
            pltpu.VMEM((4, 4, 16, 512), BF16),
            pltpu.VMEM((4, 4, 16, 512), BF16),
            pltpu.VMEM((16, 8192), F32),
            pltpu.VMEM((16, 8192), F32),
            pltpu.SemaphoreType.DMA((N_SEND,)),
            pltpu.SemaphoreType.DMA((N_RECV,)),
            pltpu.SemaphoreType.DMA((N_LOCAL,)),
        ],
        compiler_params=pltpu.CompilerParams(
            collective_id=0, has_side_effects=True, vmem_limit_bytes=60 * 1024 * 1024
        ),
        name="outer_step",
    )(at, cot, dr, outer_weights, momentum)
    return weights.reshape(4096, 512), new_outer, new_momentum


def solution(mesh):
    in_specs = (
        P("rep", "tp", None),
        P("rep", None, "tp"),
        P("rep", None, "tp"),
        P(("rep", "tp"), None),
        P(("rep", "tp"), None),
    )
    out_specs = (P(None, "tp"), P(("rep", "tp"), None), P(("rep", "tp"), None))
    return jax.shard_map(
        on_device, mesh=mesh, in_specs=in_specs, out_specs=out_specs, check_vma=False
    )
```

time: 488 us -> 185 us (0.38)
  waiting for transfers between devices: 430 us -> 0 us
  Pallas kernels: 0 us -> 176 us
  blocking collectives: 24.2 us -> 0 us
  matrix products: 14.4 us -> 0 us
  between operations: 13.8 us -> 0.66 us
    all_gather x3 -> x0, waiting for transfers between devices: 325 us -> none  [the longest x2 248 us: gathered_by_axis(): nearer = lax.all_gather(shard, axes[-1], axis=dim, tiled=True)]
    pallas_call x0 -> x1, Pallas kernels: none -> 176 us  [on_device(): pl.pallas_call(kernel, out_shape=(jax.ShapeDtypeStruct((16, 4, 4, 16, 512...]
    reduce_scatter x1 -> x0, waiting for transfers between devices: 104 us -> none  [on_device(): lax.psum_scatter(delta.astype(jnp.float32).astype(jnp.bfloat16), 'rep', s...]
    all_to_all x2 -> x0, blocking collectives: 24.2 us -> none  [the longest x1 12.9 us: on_device(): lax.all_to_all(summed.astype(jnp.bfloat16), TP, split_axis=0, concat_axis...]
    dot_general x1 -> x0, matrix products: 14.4 us -> none  [on_device(): jnp.einsum('td,tf->df', gathered_by_axis(activations, TP, 1)[0], cot_rows...]
  transfers between devices with their start and end apart: 4 -> 0, of which waited for: 4 -> 0; matrix products, arithmetic and copies ran while one was open for 0% -> 0% of each run, Pallas kernels for 0% -> 0%
where the time goes in v1:
time: 185 us
  Pallas kernels  176 us (95%)
  local copies, waits for them, and re-layouts  8.42 us (5%)
    pallas_call x1, Pallas kernels, on_device(): pl.pallas_call(kernel, out_shape=(jax.ShapeDtypeStruct((16, 4, 4, 16, 512...  176 us
    unnamed x7, local copies, waits for them, and re-layouts  6.15 us

profile of v1, /device:TPU:1, one launch (start us, length us, event | category | flops | bytes accessed | tf_op | source)
XLA Modules:
  0.0 185.0 jit_solution(4342541377142524545)
XLA Ops:
  0.6 2.3 %copy.8 = bf16[4096,128]{1,0:T(8,128)(2,1)} copy(bf16[4096,128]{0,1:T(8,128)(2,1)} %bitcast.11) | data formatting | bytes 2097152 | tf_op jit(solution)/shard_map/transpose | solution.py:337
  2.9 176.0 %outer_step.1 = (bf16[16,4,4,16,512]{4,3,2,1,0:T(8,128)(2,1)}, f32[16,8192]{1,0:T(8,128)}, f32[16,8192]{1,0:T(8,128)}) custom-call(bf16[8,2,2,128,128]{4,3,2,1,0:T(8,128)(2,1)} %bitcast.9, bf16[4,4,128,512]{3,2,1,0:T(8,128)(2,1)} %bitcast.10, bf16[8,2,2,128,512]{4,3,2,1,0:T(8,128)(2,1)} %bitcast.7, f32[16,8192]{1,0:T(8,128)} %outer.1, f32[16,8192]{1,0:T(8,128)} %mom.1), custom_call_target="tpu_custom_call" | custom-call | tf_op jit(solution)/shard_map/outer_step/pallas_call | solution.py:341
  178.9 0.0 copy-start.1
  178.9 0.0 copy-start
  178.9 4.6 %copy.12 = bf16[4096,512]{1,0:T(8,128)(2,1)} copy(bf16[4096,512]{1,0:T(8,128)(2,1)} %bitcast.8) | data formatting | bytes 8388608
  183.4 0.0 copy-done.1
  183.4 0.8 copy.13
  184.2 0.0 copy-done
  184.2 0.8 copy.14
Async XLA Ops:
  178.9 4.6 %copy-start.1 = (f32[16,8192]{1,0:T(8,128)S(1)}, f32[16,8192]{1,0:T(8,128)}, u32[]{:S(2)}) copy-start(f32[16,8192]{1,0:T(8,128)} %get-tuple-element.13) | copy-start | bytes 1572868
  178.9 5.4 %copy-start = (f32[16,8192]{1,0:T(8,128)S(1)}, f32[16,8192]{1,0:T(8,128)}, u32[]{:S(2)}) copy-start(f32[16,8192]{1,0:T(8,128)} %get-tuple-element.14) | copy-start | bytes 1572868

commit v2 on v0

v2 whole, which is shorter than its diff:
```python
import functools

import jax
import jax.numpy as jnp
from jax import lax
from jax.experimental import pallas as pl
from jax.experimental.pallas import tpu as pltpu
from jax.sharding import PartitionSpec as P

outer_rate = 0.7
nesterov = 0.9

F32 = jnp.float32
BF16 = jnp.bfloat16
MESH = pl.DeviceIdType.MESH
N_SEND = 288
N_RECV = 304
N_LOCAL = 32


def kernel(act, cot, drift, outer, mom, wout, no_out, nm_out,
           av, atv, abuf, cbuf, dbuf, pbuf, y1, y2, rbuf, zr, wbuf, obuf, mbuf,
           ss, rs, ls):
    rep = lax.axis_index("rep")
    tp = lax.axis_index("tp")
    y = rep // 4
    zhi = (rep // 2) % 2
    c = rep % 2
    x = tp // 4
    zlo = tp % 4
    z = zhi * 4 + zlo
    oc = 1 - c

    def dev(yy, zz, cc, xx):
        return ((yy % 4) * 4 + ((zz % 8) // 4) * 2 + cc, (xx % 4) * 4 + (zz % 4))

    counts = {"s": 0, "r": 0, "l": 0}
    sends = []

    def take(kind, n=1):
        base = counts[kind]
        counts[kind] += n
        return base

    def remote(src, dst, to, rsem):
        return pltpu.make_async_remote_copy(
            src_ref=src, dst_ref=dst, send_sem=ss.at[take("s")], recv_sem=rs.at[rsem],
            device_id=to, device_id_type=MESH)

    def send(src, dst, to, rsem):
        copy = remote(src, dst, to, rsem)
        copy.start()
        sends.append(copy.wait_send)

    def arrive(ref, rsem):
        pltpu.make_async_copy(ref, ref, rs.at[rsem]).wait()

    def local(src, dst):
        copy = pltpu.make_async_copy(src, dst, ls.at[take("l")])
        copy.start()
        return copy

    partner = dev(y, z, oc, x)
    up, down = dev(y + 1, z, c, x), dev(y - 1, z, c, x)
    zup, zdown = dev(y, z + 1, c, x), dev(y, z - 1, c, x)

    greeted = [dev(y, z + k, c, x) for k in (4, 3, 5, 2, 6, 1, 7)]
    greeted += [dev(y, z, c, x + 2)]
    greeted += [dev(y, z, cc, x + d) for d in (1, 3) for cc in (0, 1)]
    greeted += [up, down, partner]
    barrier = pltpu.get_barrier_semaphore()
    for other in greeted:
        pl.semaphore_signal(barrier, inc=1, device_id=other, device_id_type=MESH)

    def lanes(group, xx):
        return pl.ds(pl.multiple_of((group * 4 + xx % 4) * 128, 128), 128)

    def columns(xx):
        return pl.ds(pl.multiple_of((xx % 4) * 2048, 2048), 2048)

    a_in = local(act, av)
    c_own = local(cot.at[:, zlo], cbuf.at[zlo, c])
    d_own = local(drift.at[:, c], dbuf.at[0])
    o_own = local(outer.at[:, columns(x)], obuf.at[x])
    m_own = local(mom.at[:, columns(x)], mbuf.at[x])
    a_in.wait()
    for j in range(32):
        tile = av[:, pl.ds(j * 128, 128)].T
        for i in range(2):
            atv[j // 4, (j // 2) % 2, 2 * (j % 2) + i] = tile[i * 64:(i + 1) * 64]
    pl.semaphore_wait(barrier, len(greeted))

    a_part = take("r", 4)
    a_minus = take("r", 8)
    a_plus = take("r", 8)
    a_far = take("r", 8)
    c_part = take("r", 4)
    c_peer = take("r", 4)
    d_part = take("r", 1)
    a_own = []

    def send_a(r):
        dst = abuf.at[r, :, :, lanes(c, x)]
        send(atv.at[:, c, r], dst, dev(y, z, c, x + 1), a_minus + 2 * r + c)
        send(atv.at[:, c, r], dst, dev(y, z, c, x - 1), a_plus + 2 * r + c)
        send(atv.at[:, oc, r], dst, dev(y, z, oc, x + 1), a_minus + 2 * r + c)
        send(atv.at[:, oc, r], dst, dev(y, z, oc, x - 1), a_plus + 2 * r + c)
        send(atv.at[:, oc, r], dst, partner, a_part + r)
        a_own.append(local(atv.at[:, c, r], dst))

    def forward_a(r):
        for group in range(2):
            arrive(abuf.at[r, :, :, lanes(group, x - 1)], a_minus + 2 * r + group)
        src = abuf.at[r, :, :, lanes(0, x - 1)]
        send(src, src, dev(y, z, c, x + 1), a_far + 2 * r)
        for group in range(2):
            arrive(abuf.at[r, :, :, lanes(group, x + 1)], a_plus + 2 * r + group)
        src = abuf.at[r, :, :, lanes(1, x + 1)]
        send(src, src, dev(y, z, c, x - 1), a_far + 2 * r + 1)

    def finish_a(r):
        a_own[r].wait()
        arrive(abuf.at[r, :, :, lanes(oc, x)], a_part + r)
        for group in range(2):
            arrive(abuf.at[r, :, :, lanes(group, x + 2)], a_far + 2 * r + group)

    def block_of(s, at=None):
        at = zlo if at is None else at
        pair = at // 2
        low = at % 2
        return (at, 2 * pair + 1 - low, 3 - at, 2 * (1 - pair) + low)[s]

    def send_c(s):
        if s == 0:
            send(cot.at[:, zlo], cbuf.at[zlo, c], partner, c_part)
        else:
            to = block_of(s)
            send(cot.at[:, to], cbuf.at[zlo, c], dev(y, zhi * 4 + to, c, x), c_peer + s)

    def send_d():
        send(drift.at[:, oc], dbuf.at[1], partner, d_part)

    def ready_c(s):
        q = block_of(s)
        if s == 0:
            c_own.wait()
        else:
            arrive(cbuf.at[q, c], c_peer + s)
            send(cbuf.at[q, c], cbuf.at[q, c], partner, c_part + s)
        arrive(cbuf.at[q, oc], c_part + s)

    y_first = take("r", 32)
    y_plain = take("r", 32)
    y_sum = take("r", 32)

    def compute(r, s):
        unit = r * 4 + s
        q = block_of(s)
        if r == 0:
            ready_c(s)
        if r == 0 and s == 0:
            d_own.wait()
            arrive(dbuf.at[1], d_part)
        lhs = abuf[r].reshape(512, 1024)
        rhs = cbuf[q].reshape(1024, 512)
        total = jnp.dot(lhs, rhs, preferred_element_type=F32)
        if s == 0:
            total = total + dbuf[0, :, r].reshape(512, 512).astype(F32)
            total = total + dbuf[1, :, r].reshape(512, 512).astype(F32)
        pbuf[r, s] = total.astype(BF16).reshape(4, 2, 64, 512)
        far, near, back = (y + 2) % 4, (y + 1) % 4, (y + 3) % 4
        send(pbuf.at[r, s, far, 0], y1.at[0, r, s], up, y_first + unit)
        send(pbuf.at[r, s, far, 1], y1.at[1, r, s], down, y_first + 16 + unit)
        send(pbuf.at[r, s, near, 1], y2.at[0, r, s, 1], up, y_plain + unit)
        send(pbuf.at[r, s, back, 0], y2.at[1, r, s, 0], down, y_plain + 16 + unit)

    def relay_y(r, s):
        unit = r * 4 + s
        near, back = (y + 1) % 4, (y + 3) % 4
        arrive(y1.at[0, r, s], y_first + unit)
        pbuf[r, s, near, 0] = (pbuf[r, s, near, 0].astype(F32) + y1[0, r, s].astype(F32)).astype(BF16)
        send(pbuf.at[r, s, near, 0], y2.at[0, r, s, 0], up, y_sum + unit)
        arrive(y1.at[1, r, s], y_first + 16 + unit)
        pbuf[r, s, back, 1] = (pbuf[r, s, back, 1].astype(F32) + y1[1, r, s].astype(F32)).astype(BF16)
        send(pbuf.at[r, s, back, 1], y2.at[1, r, s, 1], down, y_sum + 16 + unit)

    def finish_y(r, s):
        unit = r * 4 + s
        q = block_of(s)
        arrive(y2.at[0, r, s, 1], y_plain + unit)
        arrive(y2.at[1, r, s, 0], y_plain + 16 + unit)
        arrive(y2.at[0, r, s, 0], y_sum + unit)
        arrive(y2.at[1, r, s, 1], y_sum + 16 + unit)
        for hi in range(2):
            total = (pbuf[r, s, y, hi].astype(F32) + y2[0, r, s, hi].astype(F32)
                     + y2[1, r, s, hi].astype(F32)).astype(BF16)
            for pz in range(4):
                rbuf[r, hi * 4 + pz, q] = total[pz * 16:(pz + 1) * 16]

    z_up = take("r", 16)
    z_down = take("r", 16)

    def ring_z(r, step):
        lo, hi = pl.ds(0, 2), pl.ds(2, 2)
        if step == 0:
            far = (z + 4) % 8
            send(rbuf.at[r, far, lo], zr.at[0, r, 0, lo], zup, z_up + 4 * r)
            send(rbuf.at[r, far, hi], zr.at[1, r, 0, hi], zdown, z_down + 4 * r)
            return
        for way, (base, to) in enumerate(((z_up, zup), (z_down, zdown))):
            part = (lo, hi)[way] if step == 1 else pl.ds(0, 4)
            arrive(zr.at[way, r, step - 1, part], base + 4 * r + step - 1)
            if step < 4:
                target = (z + (4 - step)) % 8 if way == 0 else (z + 4 + step) % 8
                rbuf[r, target, part] = (rbuf[r, target, part].astype(F32)
                                         + zr[way, r, step - 1, part].astype(F32)).astype(BF16)
                send(rbuf.at[r, target], zr.at[way, r, step], to, base + 4 * r + step)

    def skip_z(step):
        halves = pl.ds(0, 2), pl.ds(2, 2)
        for way, base in enumerate((z_up, z_down)):
            sign = 1 - 2 * way
            one, two = (z + 8 + sign) % 8, (z + 8 + 2 * sign) % 8
            half = halves[way]
            if step == 0:
                to = dev(y, two, c, x)
                send(rbuf.at[3, (z + 4) % 8, half], zr.at[way, 3, 0, half], to, base + 12)
                send(rbuf.at[3, (z + 8 + 3 * sign) % 8], zr.at[way, 3, 1], to, base + 13)
            elif step == 1:
                arrive(zr.at[way, 3, 0, half], base + 12)
                rbuf[3, two, half] = (rbuf[3, two, half].astype(F32)
                                      + zr[way, 3, 0, half].astype(F32)).astype(BF16)
                send(rbuf.at[3, two], zr.at[way, 3, 2], dev(y, two, c, x), base + 14)
                arrive(zr.at[way, 3, 1], base + 13)
                rbuf[3, one] = (rbuf[3, one].astype(F32)
                                + zr[way, 3, 1].astype(F32)).astype(BF16)
                send(rbuf.at[3, one], zr.at[way, 3, 3], dev(y, one, c, x), base + 15)
            else:
                arrive(zr.at[way, 3, 2], base + 14)
                arrive(zr.at[way, 3, 3], base + 15)

    s_out = take("r", 4)
    s_mom = take("r", 4)

    def send_state():
        for d in (1, 3, 2):
            xx = (x + d) % 4
            send(outer.at[:, columns(xx)], obuf.at[x], dev(y, z, c, xx), s_out + d)
            send(mom.at[:, columns(xx)], mbuf.at[x], dev(y, z, c, xx), s_mom + d)

    def finish_state():
        o_own.wait()
        m_own.wait()
        for d in (1, 3, 2):
            arrive(obuf.at[(x - d) % 4], s_out + d)
            arrive(mbuf.at[(x - d) % 4], s_mom + d)

    b_out = take("r", 4)
    b_mom = take("r", 4)
    r_two = take("r", 32)
    w_own = []

    def update(r):
        for q in range(4):
            cols = pl.ds(q * 512, 512)
            total = rbuf[r, z, q].astype(F32)
            for way in range(2):
                for step in ((3,), (2, 3))[r == 3]:
                    total = total + zr[way, r, step, q].astype(F32)
            average = total / 16
            momentum = nesterov * mbuf[r, :, cols] + average
            weights = obuf[r, :, cols] - outer_rate * (average + nesterov * momentum)
            mbuf[r, :, cols] = momentum
            obuf[r, :, cols] = weights
            wbuf[r, q] = weights.astype(BF16)
        own = wout.at[y, zhi, c, r, zlo]
        for k in (4, 3, 5, 2, 6, 1, 7):
            zz = (z + k) % 8
            send(wbuf.at[r, zz % 4], own, dev(y, zz, c, x), r_two + 8 * r + k)
        w_own.append(local(wbuf.at[r, zlo], own))
        backs = [remote(buf.at[r], out.at[:, columns(x)], dev(y, z, c, r), base + x)
                 for buf, out, base in ((obuf, no_out, b_out), (mbuf, nm_out, b_mom))]
        keeps = [pltpu.make_async_copy(buf.at[r], out.at[:, columns(x)], ls.at[take("l")])
                 for buf, out in ((obuf, no_out), (mbuf, nm_out))]

        @pl.when(x != r)
        def _():
            for copy in backs:
                copy.start()

        @pl.when(x == r)
        def _():
            for copy in keeps:
                copy.start()

        def finish():
            @pl.when(x != r)
            def _():
                for copy in backs:
                    copy.wait_send()

            @pl.when(x == r)
            def _():
                for copy in keeps:
                    copy.wait()

        sends.append(finish)

    r_up = take("r", 4)
    r_down = take("r", 4)
    r_far = take("r", 8)
    r_part = take("r", 20)

    def gather_own(r):
        w_own[r].wait()
        for k in (1, 7, 2, 6, 3, 5, 4):
            zz = (z - k) % 8
            arrive(wout.at[y, zz // 4, c, r, zz % 4], r_two + 8 * r + k)
        src = wout.at[y, :, c, r]
        send(src, src, up, r_down + r)
        send(src, src, down, r_up + r)
        send(src, src, partner, r_part + 5 * r)

    def gather_near(r):
        back, near = (y + 3) % 4, (y + 1) % 4
        src = wout.at[back, :, c, r]
        arrive(src, r_down + r)
        send(wout.at[back, 0, c, r], wout.at[back, 0, c, r], up, r_far + 2 * r)
        send(src, src, partner, r_part + 5 * r + 1)
        src = wout.at[near, :, c, r]
        arrive(src, r_up + r)
        send(wout.at[near, 1, c, r], wout.at[near, 1, c, r], down, r_far + 2 * r + 1)
        send(src, src, partner, r_part + 5 * r + 2)

    def gather_far(r):
        for half in range(2):
            src = wout.at[(y + 2) % 4, half, c, r]
            arrive(src, r_far + 2 * r + half)
            send(src, src, partner, r_part + 5 * r + 3 + half)

    def gather_done(r):
        arrive(wout.at[y, :, oc, r], r_part + 5 * r)
        arrive(wout.at[(y + 3) % 4, :, oc, r], r_part + 5 * r + 1)
        arrive(wout.at[(y + 1) % 4, :, oc, r], r_part + 5 * r + 2)
        for half in range(2):
            arrive(wout.at[(y + 2) % 4, half, oc, r], r_part + 5 * r + 3 + half)

    send_a(0)
    send_c(0)
    send_c(1)
    send_c(2)
    send_d()
    forward_a(0)
    send_a(1)
    finish_a(0)

    units = ((0, 0), (0, 1), (1, 0), (1, 1), (0, 2), (1, 2), (2, 0), (2, 1),
             (2, 2), (0, 3), (1, 3), (2, 3), (3, 0), (3, 1), (3, 2), (3, 3))

    def slot(i):
        if 1 <= i < 17:
            relay_y(*units[i - 1])
        if 3 <= i:
            finish_y(*units[i - 3])

    compute(0, 0)
    compute(0, 1)
    slot(1)
    forward_a(1)
    send_a(2)
    finish_a(1)
    send_c(3)
    compute(1, 0)
    slot(2)
    compute(1, 1)
    slot(3)
    compute(0, 2)
    forward_a(2)
    send_a(3)
    send_state()
    slot(4)
    compute(1, 2)
    slot(5)
    finish_a(2)
    compute(2, 0)
    slot(6)
    compute(2, 1)
    slot(7)
    forward_a(3)
    compute(2, 2)
    slot(8)
    compute(0, 3)
    relay_y(2, 2)
    finish_y(2, 0)
    compute(1, 3)
    relay_y(0, 3)
    finish_y(2, 1)
    compute(2, 3)
    finish_a(3)
    compute(3, 0)
    relay_y(1, 3)
    finish_y(2, 2)
    finish_y(0, 3)
    ring_z(0, 0)
    compute(3, 1)
    relay_y(2, 3)
    finish_y(1, 3)
    ring_z(1, 0)
    ring_z(0, 1)
    compute(3, 2)
    relay_y(3, 0)
    finish_y(2, 3)
    ring_z(2, 0)
    ring_z(0, 2)
    ring_z(1, 1)
    compute(3, 3)
    relay_y(3, 1)
    finish_y(3, 0)
    ring_z(0, 3)
    ring_z(1, 2)
    ring_z(2, 1)
    relay_y(3, 2)
    finish_y(3, 1)
    ring_z(0, 4)
    finish_state()
    update(0)
    ring_z(1, 3)
    ring_z(2, 2)
    relay_y(3, 3)
    finish_y(3, 2)
    ring_z(1, 4)
    update(1)
    ring_z(2, 3)
    finish_y(3, 3)
    skip_z(0)
    ring_z(2, 4)
    update(2)
    gather_own(0)
    gather_own(1)
    skip_z(1)
    gather_near(0)
    gather_near(1)
    gather_own(2)
    skip_z(2)
    update(3)
    gather_far(0)
    gather_far(1)
    gather_near(2)
    gather_own(3)
    gather_far(2)
    gather_done(0)
    gather_done(1)
    gather_near(3)
    gather_done(2)
    gather_far(3)
    gather_done(3)
    for d in (1, 3, 2):
        xx = (x - d) % 4
        arrive(no_out.at[:, columns(xx)], b_out + xx)
        arrive(nm_out.at[:, columns(xx)], b_mom + xx)
    for finish in sends:
        finish()


def on_device(activations, cotangent, drift, outer_weights, momentum):
    cot = cotangent[0].reshape(4, 4, 128, 512)
    dr = drift[0].reshape(8, 2, 4, 64, 512)
    any_spec = pl.BlockSpec(memory_space=pl.ANY)
    hbm_spec = pl.BlockSpec(memory_space=pltpu.HBM)
    weights, new_outer, new_momentum = pl.pallas_call(
        kernel,
        out_shape=(
            pltpu.VMEM((4, 2, 2, 4, 4, 16, 512), BF16),
            pltpu.VMEM((16, 8192), F32),
            pltpu.VMEM((16, 8192), F32),
        ),
        in_specs=[hbm_spec] * 5,
        out_specs=[any_spec] * 3,
        scratch_shapes=[
            pltpu.VMEM((128, 4096), BF16),
            pltpu.VMEM((8, 2, 4, 64, 128), BF16),
            pltpu.VMEM((4, 8, 64, 1024), BF16),
            pltpu.VMEM((4, 2, 4, 128, 512), BF16),
            pltpu.VMEM((2, 8, 4, 64, 512), BF16),
            pltpu.VMEM((4, 4, 4, 2, 64, 512), BF16),
            pltpu.VMEM((2, 4, 4, 64, 512), BF16),
            pltpu.VMEM((2, 4, 4, 2, 64, 512), BF16),
            pltpu.VMEM((4, 8, 4, 16, 512), BF16),
            pltpu.VMEM((2, 4, 4, 4, 16, 512), BF16),
            pltpu.VMEM((4, 4, 16, 512), BF16),
            pltpu.VMEM((4, 16, 2048), F32),
            pltpu.VMEM((4, 16, 2048), F32),
            pltpu.SemaphoreType.DMA((N_SEND,)),
            pltpu.SemaphoreType.DMA((N_RECV,)),
            pltpu.SemaphoreType.DMA((N_LOCAL,)),
        ],
        compiler_params=pltpu.CompilerParams(
            collective_id=0, has_side_effects=True, vmem_limit_bytes=54 * 1024 * 1024
        ),
        name="outer_step",
    )(activations[0], cot, dr, outer_weights, momentum)
    return weights.reshape(4096, 512), new_outer, new_momentum


def solution(mesh):
    in_specs = (
        P("rep", "tp", None),
        P("rep", None, "tp"),
        P("rep", None, "tp"),
        P(("rep", "tp"), None),
        P(("rep", "tp"), None),
    )
    out_specs = (P(None, "tp"), P(("rep", "tp"), None), P(("rep", "tp"), None))
    return jax.shard_map(
        on_device, mesh=mesh, in_specs=in_specs, out_specs=out_specs, check_vma=False
    )
```

time: 488 us -> 144 us (0.30)
  waiting for transfers between devices: 430 us -> 0 us
  Pallas kernels: 0 us -> 139 us
  blocking collectives: 24.2 us -> 0 us
  matrix products: 14.4 us -> 0 us
  between operations: 13.8 us -> 0.64 us
    all_gather x3 -> x0, waiting for transfers between devices: 325 us -> none  [the longest x2 248 us: gathered_by_axis(): nearer = lax.all_gather(shard, axes[-1], axis=dim, tiled=True)]
    pallas_call x0 -> x1, Pallas kernels: none -> 139 us  [on_device(): pl.pallas_call(kernel, out_shape=(pltpu.VMEM((4, 2, 2, 4, 4, 16, 512), BF...]
    reduce_scatter x1 -> x0, waiting for transfers between devices: 104 us -> none  [on_device(): lax.psum_scatter(delta.astype(jnp.float32).astype(jnp.bfloat16), 'rep', s...]
    all_to_all x2 -> x0, blocking collectives: 24.2 us -> none  [the longest x1 12.9 us: on_device(): lax.all_to_all(summed.astype(jnp.bfloat16), TP, split_axis=0, concat_axis...]
    dot_general x1 -> x0, matrix products: 14.4 us -> none  [on_device(): jnp.einsum('td,tf->df', gathered_by_axis(activations, TP, 1)[0], cot_rows...]
  transfers between devices with their start and end apart: 4 -> 0, of which waited for: 4 -> 0; matrix products, arithmetic and copies ran while one was open for 0% -> 0% of each run, Pallas kernels for 0% -> 0%
where the time goes in v2:
time: 144 us
  Pallas kernels  139 us (97%)
  local copies, waits for them, and re-layouts  3.6 us (2%)
    pallas_call x1, Pallas kernels, on_device(): pl.pallas_call(kernel, out_shape=(pltpu.VMEM((4, 2, 2, 4, 4, 16, 512), BF...  139 us
    unnamed x3, local copies, waits for them, and re-layouts  3.6 us

profile of v2, /device:TPU:1, one launch (start us, length us, event | category | flops | bytes accessed | tf_op | source)
XLA Modules:
  0.0 143.5 jit_solution(3362650347082284827)
XLA Ops:
  0.6 139.3 %outer_step.1 = (bf16[4,2,2,4,4,16,512]{6,5,4,3,2,1,0:T(8,128)(2,1)S(1)}, f32[16,8192]{1,0:T(8,128)S(1)}, f32[16,8192]{1,0:T(8,128)S(1)}) custom-call(bf16[128,4096]{1,0:T(8,128)(2,1)} %bitcast.7, bf16[4,4,128,512]{3,2,1,0:T(8,128)(2,1)} %bitcast.6, bf16[8,2,4,64,512]{4,3,2,1,0:T(8,128)(2,1)} %bitcast.5, f32[16,8192]{1,0:T(8,128)} %outer.1, f32[16,8192]{1,0:T(8,128)} %mom.1), custom_call_target="tpu_custom_call" | custom-call | tf_op jit(solution)/shard_map/outer_step/pallas_call | solution.py:470
  139.9 2.0 %copy.11 = bf16[4096,512]{1,0:T(8,128)(2,1)} copy(bf16[4096,512]{1,0:T(8,128)(2,1)S(1)} %bitcast.4) | data formatting | bytes 8388608
  141.9 0.8 copy.12
  142.7 0.8 copy.13

commit v3 on v0

v3 whole, which is shorter than its diff:
```python
import functools

import jax
import jax.numpy as jnp
from jax import lax
from jax.experimental import pallas as pl
from jax.experimental.pallas import tpu as pltpu
from jax.sharding import PartitionSpec as P

outer_rate = 0.7
nesterov = 0.9

F32 = jnp.float32
BF16 = jnp.bfloat16
MESH = pl.DeviceIdType.MESH
POOL = 72
N_RECV = 192
N_LOCAL = 16

ACTS = (12.5, 23.5, 35.0, 47.0)
COTS = ((1.0, 13.0, 16.0, 28.0), (1.0, 24.0, 41.0, 50.0))
PACE = 2.08


def reduction_order():
    waiting = [(h * 4 + r, s, max(ACTS[r], COTS[h][s]))
               for h in range(2) for r in range(4) for s in range(4)]
    now, order = 0.0, []
    while waiting:
        now = max(now, min(ready for _, _, ready in waiting))
        unit = next(u for u in waiting if u[2] <= now)
        waiting.remove(unit)
        order.append((unit[0], unit[1], unit[2], now))
        now += PACE
    return order


def kernel(act, cot, drift, outer, mom, wout, no_out, nm_out,
           av, atv, abuf, cbuf, dbuf, pbuf, y1, y2, rbuf, zr, wbuf, obuf, mbuf, tloc, tbuf, fbuf, xr,
           ss, rs, ls):
    rep = lax.axis_index("rep")
    tp = lax.axis_index("tp")
    y = rep // 4
    zhi = (rep // 2) % 2
    c = rep % 2
    x = tp // 4
    zlo = tp % 4
    z = zhi * 4 + zlo
    oc = 1 - c

    def dev(yy, zz, cc, xx):
        return ((yy % 4) * 4 + ((zz % 8) // 4) * 2 + cc, (xx % 4) * 4 + (zz % 4))

    counts = {"s": 0, "r": 0, "l": 0}
    sends = []

    def take(kind, n=1):
        base = counts[kind]
        counts[kind] += n
        return base

    def remote(src, dst, to, rsem, ssem):
        return pltpu.make_async_remote_copy(
            src_ref=src, dst_ref=dst, send_sem=ss.at[ssem], recv_sem=rs.at[rsem],
            device_id=to, device_id_type=MESH)

    def send(src, dst, to, rsem):
        if len(sends) == POOL:
            sends.pop(0)()
        copy = remote(src, dst, to, rsem, take("s") % POOL)
        copy.start()
        sends.append(copy.wait_send)

    def arrive(ref, rsem):
        pltpu.make_async_copy(ref, ref, rs.at[rsem]).wait()

    def local(src, dst):
        copy = pltpu.make_async_copy(src, dst, ls.at[take("l")])
        copy.start()
        return copy

    partner = dev(y, z, oc, x)
    up, down = dev(y + 1, z, c, x), dev(y - 1, z, c, x)
    zup, zdown = dev(y, z + 1, c, x), dev(y, z - 1, c, x)

    greeted = [dev(y, z + k, c, x) for k in (4, 3, 5, 2, 6, 1, 7)]
    greeted += [dev(y, z, c, x + 2)]
    greeted += [dev(y, z, cc, x + d) for d in (1, 3) for cc in (0, 1)]
    greeted += [up, down, partner]
    barrier = pltpu.get_barrier_semaphore()
    for other in greeted:
        pl.semaphore_signal(barrier, inc=1, device_id=other, device_id_type=MESH)

    def lanes(group, xx):
        return pl.ds(pl.multiple_of((group * 4 + xx % 4) * 128, 128), 128)

    def columns(xx):
        return pl.ds(pl.multiple_of((xx % 4) * 2048, 2048), 2048)

    a_in = local(act, av)
    c_own = local(cot.at[:, zlo], cbuf.at[zlo, c])
    d_own = local(drift.at[:, c], dbuf.at[0])
    o_own = local(outer, obuf)
    m_own = local(mom, mbuf)
    a_in.wait()
    for j in range(32):
        tile = av[:, pl.ds(j * 128, 128)].T
        for i in range(2):
            atv[j // 4, (j // 2) % 2, 2 * (j % 2) + i] = tile[i * 64:(i + 1) * 64]
    pl.semaphore_wait(barrier, len(greeted))

    a_part = take("r", 4)
    a_minus = take("r", 8)
    a_plus = take("r", 8)
    a_far = take("r", 8)
    c_part = take("r", 8)
    c_peer = take("r", 8)
    d_part = take("r", 1)
    a_own = []

    def send_a(r):
        dst = abuf.at[r, :, :, lanes(c, x)]
        for turn in range(2):
            ahead = 1 - 2 * c if turn == 0 else 2 * c - 1
            rsem = a_minus + 2 * r + c + 8 * (c if turn == 0 else oc)
            send(atv.at[:, c, r], dst, dev(y, z, c, x + 4 + ahead), rsem)
            send(atv.at[:, oc, r], dst, dev(y, z, oc, x + 4 + ahead), rsem)
        send(atv.at[:, oc, r], dst, partner, a_part + r)
        a_own.append(local(atv.at[:, c, r], dst))

    def forward_a(r):
        src = abuf.at[r, :, :, lanes(0, x + 3)]
        arrive(src, a_minus + 2 * r)
        send(src, src, dev(y, z, c, x + 1), a_far + 2 * r)
        src = abuf.at[r, :, :, lanes(1, x + 1)]
        arrive(src, a_plus + 2 * r + 1)
        send(src, src, dev(y, z, c, x + 3), a_far + 2 * r + 1)

    def finish_a(r):
        a_own[r].wait()
        arrive(abuf.at[r, :, :, lanes(oc, x)], a_part + r)
        arrive(abuf.at[r, :, :, lanes(1, x + 3)], a_minus + 2 * r + 1)
        arrive(abuf.at[r, :, :, lanes(0, x + 1)], a_plus + 2 * r)
        for group in range(2):
            arrive(abuf.at[r, :, :, lanes(group, x + 2)], a_far + 2 * r + group)

    def block_of(s, at=None):
        at = zlo if at is None else at
        pair = at // 2
        low = at % 2
        return (at, 2 * pair + 1 - low, 3 - at, 2 * (1 - pair) + low)[s]

    def half(h):
        return pl.ds(256 * h, 256)

    def send_c(h, s):
        dst = cbuf.at[zlo, c, :, :, half(h)]
        if s == 0:
            send(cot.at[:, zlo, :, half(h)], dst, partner, c_part + 4 * h)
        else:
            to = block_of(s)
            send(cot.at[:, to, :, half(h)], dst, dev(y, zhi * 4 + to, c, x), c_peer + 4 * h + s)

    def send_d():
        send(drift.at[:, oc], dbuf.at[1], partner, d_part)

    def pass_c(h, s):
        src = cbuf.at[block_of(s), c, :, :, half(h)]
        arrive(src, c_peer + 4 * h + s)
        send(src, src, partner, c_part + 4 * h + s)

    def finish_c(h, s):
        if h == 0 and s == 0:
            c_own.wait()
        arrive(cbuf.at[block_of(s), oc, :, :, half(h)], c_part + 4 * h + s)

    have = set()

    def once(step, *args):
        if (step, args) not in have:
            have.add((step, args))
            step(*args)

    def cut(n):
        return n % 4, half(n // 4)

    y_first = take("r", 32)
    y_all = take("r", 32)

    def finish_d():
        d_own.wait()
        arrive(dbuf.at[1], d_part)

    def compute(n, s):
        unit = n * 4 + s
        r, cols = cut(n)
        wide = 256
        q = block_of(s)
        once(finish_a, r)
        once(finish_c, n // 4, s)
        once(finish_d)
        lhs = abuf[r].reshape(512, 1024)
        rhs = cbuf[q, :, :, :, cols].reshape(1024, wide)
        total = jnp.dot(lhs, rhs, preferred_element_type=F32)
        if s == 0:
            total = total + dbuf[0, :, r, :, cols].reshape(512, wide).astype(F32)
            total = total + dbuf[1, :, r, :, cols].reshape(512, wide).astype(F32)
        pbuf[r, s, :, :, :, cols] = total.astype(BF16).reshape(4, 2, 64, wide)
        far, near, back = (y + 2) % 4, (y + 1) % 4, (y + 3) % 4
        send(pbuf.at[r, s, far, 0, :, cols], y1.at[0, r, s, :, cols], up, y_first + unit)
        send(pbuf.at[r, s, far, 1, :, cols], y1.at[1, r, s, :, cols], down, y_first + unit)
        send(pbuf.at[r, s, near, 1, :, cols], y2.at[0, r, s, 1, :, cols], up, y_all + unit)
        send(pbuf.at[r, s, back, 0, :, cols], y2.at[1, r, s, 0, :, cols], down, y_all + unit)

    def relay_y(n, s):
        unit = n * 4 + s
        r, cols = cut(n)
        arrive(y1.at[:, r, s, :, cols], y_first + unit)
        for way, yy in enumerate(((y + 1) % 4, (y + 3) % 4)):
            part = pbuf.at[r, s, yy, way, :, cols]
            came = y1.at[way, r, s, :, cols]
            part[...] = (part[...].astype(F32) + came[...].astype(F32)).astype(BF16)
            send(part, y2.at[way, r, s, way, :, cols], (up, down)[way], y_all + unit)

    def finish_y(n, s):
        unit = n * 4 + s
        r, cols = cut(n)
        q = block_of(s)
        arrive(y2.at[:, r, s, :, :, cols], y_all + unit)
        for hi in range(2):
            total = (pbuf[r, s, y, hi, :, cols].astype(F32) + y2[0, r, s, hi, :, cols].astype(F32)
                     + y2[1, r, s, hi, :, cols].astype(F32)).astype(BF16)
            for pz in range(4):
                rbuf[r, hi * 4 + pz, q, :, cols] = total[pz * 16:(pz + 1) * 16]

    z_in = take("r", 32)

    def skip_z(step):
        cols = half(1)
        every = pl.ds(0, 4)
        base = z_in + 28
        if step == 1:
            arrive(zr.at[0, 3, 0, :, :, cols], base)
            arrive(zr.at[:, 3, 1, :, :, cols], base + 1)
        elif step == 2:
            arrive(zr.at[:, 3, 2, :, :, cols], base + 2)
            arrive(zr.at[:, 3, 3, :, :, cols], base + 3)
            return
        for way in range(2):
            sign = 1 - 2 * way
            one, two = (z + 8 + sign) % 8, (z + 8 + 2 * sign) % 8
            some = pl.ds(2 * way, 2)
            first = zr.at[0, 3, 0, some, :, cols]
            second = zr.at[way, 3, 1, :, :, cols]

            def held(zz, part=every):
                return rbuf.at[3, zz % 8, part, :, cols]

            if step == 0:
                to = dev(y, two, c, x)
                send(held(z + 4, some), first, to, base)
                send(held(z + 8 + 3 * sign), second, to, base + 1)
                continue
            for i, (zz, part, came) in enumerate(((two, some, first), (one, every, second))):
                own = held(zz, part)
                own[...] = (own[...].astype(F32) + came[...].astype(F32)).astype(BF16)
                send(held(zz), zr.at[way, 3, 2 + i, :, :, cols], dev(y, zz, c, x), base + 2 + i)

    def ring_z(n, step):
        if n == 7:
            skip_z(step)
            return
        r, cols = cut(n)
        base = z_in + 4 * n + step
        if step == 1:
            arrive(zr.at[0, r, 0, :, :, cols], base - 1)
        elif step > 1:
            arrive(zr.at[:, r, step - 1, :, :, cols], base - 1)
        if step == 4:
            return
        for way in range(2):
            to = (zup, zdown)[way]
            some = pl.ds(2 * way, 2)
            if step == 0:
                send(rbuf.at[r, (z + 4) % 8, some, :, cols], zr.at[0, r, 0, some, :, cols], to, base)
                continue
            target = (z + (4 - step)) % 8 if way == 0 else (z + 4 + step) % 8
            if step == 1:
                came, own = zr.at[0, r, 0, some, :, cols], rbuf.at[r, target, some, :, cols]
            else:
                came, own = zr.at[way, r, step - 1, :, :, cols], rbuf.at[r, target, :, :, cols]
            own[...] = (own[...].astype(F32) + came[...].astype(F32)).astype(BF16)
            send(rbuf.at[r, target, :, :, cols], zr.at[way, r, step, :, :, cols], to, base)

    s_in = take("r", 4)

    def send_state():
        o_own.wait()
        m_own.wait()
        tloc[...] = obuf[...] - outer_rate * nesterov * nesterov * mbuf[...]
        for d in (1, 3, 2):
            xx = (x + d) % 4
            send(tloc.at[:, columns(xx)], tbuf.at[x], dev(y, z, c, xx), s_in + d)
        tbuf[x] = tloc[:, columns(x)]

    def finish_state():
        for d in (1, 3, 2):
            arrive(tbuf.at[(x - d) % 4], s_in + d)

    b_in = take("r", 2)
    r_two = take("r", 8)

    def update(n):
        r, cut_cols = cut(n)
        first, wide = 256 * (n // 4), 256
        once(finish_state)
        for q in range(4):
            cols = pl.ds(q * 512 + first, wide)
            total = rbuf[r, z, q, :, cut_cols].astype(F32)
            for way in range(2):
                for step in ((3,), (2, 3))[n == 7]:
                    total = total + zr[way, r, step, q, :, cut_cols].astype(F32)
            fbuf[r, q, :, cut_cols] = total.astype(BF16)
            average = fbuf[r, q, :, cut_cols].astype(F32) / 16
            weights = tbuf[r, :, cols] - outer_rate * (1 + nesterov) * average
            wbuf[r, q, :, cut_cols] = weights.astype(BF16)
        own = wout.at[y, zhi, c, r, zlo, :, cut_cols]
        for k in (4, 3, 5, 2, 6, 1, 7):
            zz = (z + k) % 8
            send(wbuf.at[r, zz % 4, :, cut_cols], own, dev(y, zz, c, x), r_two + n)
        pltpu.make_async_copy(wbuf.at[r, zlo, :, cut_cols], own, rs.at[r_two + n]).start()
        src, dst = fbuf.at[r, :, :, cut_cols], xr.at[x, :, :, cut_cols]
        back = remote(src, dst, dev(y, z, c, r), b_in + n // 4, POOL + n)
        keep = pltpu.make_async_copy(src, dst, rs.at[b_in + n // 4])

        @pl.when(x != r)
        def _():
            back.start()

        @pl.when(x == r)
        def _():
            keep.start()

        def finish_back():
            @pl.when(x != r)
            def _():
                back.wait_send()

        kept.append(finish_back)

    kept = []

    def finish_outer():
        for finish in kept:
            finish()
        for h in range(2):
            arrive(xr.at[:, :, :, half(h)], b_in + h)
        for xx in range(4):
            for q in range(4):
                cols = pl.ds((xx * 4 + q) * 512, 512)
                average = xr[xx, q].astype(F32) / 16
                momentum = nesterov * mbuf[:, cols] + average
                nm_out[:, cols] = momentum
                no_out[:, cols] = obuf[:, cols] - outer_rate * (average + nesterov * momentum)

    r_up = take("r", 8)
    r_down = take("r", 8)
    r_far = take("r", 8)
    r_part = take("r", 8)

    def both(n, yy, cc):
        r, cols = cut(n)
        return wout.at[yy, :, cc, r, :, :, cols]

    def one_of(n, yy, hi, cc):
        r, cols = cut(n)
        return wout.at[yy, hi, cc, r, :, :, cols]

    def gather_own(n):
        arrive(both(n, y, c), r_two + n)
        src = both(n, y, c)
        send(src, src, up, r_down + n)
        send(src, src, down, r_up + n)
        send(src, src, partner, r_part + n)

    def gather_near(n):
        for way, yy in enumerate(((y + 3) % 4, (y + 1) % 4)):
            src = both(n, yy, c)
            arrive(src, (r_down, r_up)[way] + n)
            nearer = one_of(n, yy, way, c)
            send(nearer, nearer, (up, down)[way], r_far + n)
            send(src, src, partner, r_part + n)

    def gather_far(n):
        src = both(n, (y + 2) % 4, c)
        arrive(src, r_far + n)
        send(src, src, partner, r_part + n)

    def gather_done(n):
        r, cols = cut(n)
        arrive(wout.at[:, :, oc, r, :, :, cols], r_part + n)

    plan = [
        (0.0, send_a, 0), (0.0, send_c, 0, 0), (0.0, send_c, 0, 1), (0.0, send_c, 0, 2),
        (0.0, send_d), (0.0, send_c, 1, 0), (7.5, forward_a, 0), (7.5, send_a, 1), (7.6, send_c, 0, 3),
        (12.4, send_c, 1, 1), (18.0, forward_a, 1), (18.0, send_a, 2), (18.1, send_c, 1, 2),
        (23.5, send_c, 1, 3), (28.8, forward_a, 2), (28.8, send_a, 3), (28.9, send_state), (40.0, forward_a, 3),
    ]
    for h in range(2):
        for s in range(1, 4):
            plan.append((COTS[h][s] - 1.5, pass_c, h, s))
    ended = [0.0] * 8
    for n, s, ready, begun in reduction_order():
        plan.append((max(ready, begun - 3.0), compute, n, s))
        plan.append((begun + 4.2, relay_y, n, s))
        plan.append((begun + 8.4, finish_y, n, s))
        ended[n] = max(ended[n], begun + 8.5)
    ring = 45.0
    for n in range(8):
        ring = max(ended[n] + 0.8, ring + 4.0)
        pace, steps = (4.2, 4) if n < 7 else (5.5, 2)
        for step in range(steps + 1):
            plan.append((ring + pace * step, ring_z, n, step))
        stop = ring + pace * steps + 0.1
        begin = max(stop + 4.8, 84.0 + 1.5 * n)
        for when, step in ((stop, update), (begin, gather_own), (begin + 4.4, gather_near),
                           (begin + 8.2, gather_far), (150.0, gather_done)):
            plan.append((when, step, n))
    plan.append((149.0, finish_outer))
    plan.sort(key=lambda entry: entry[0])
    for _, step, *args in plan:
        step(*args)

    for finish in sends:
        finish()


def on_device(activations, cotangent, drift, outer_weights, momentum):
    cot = cotangent[0].reshape(4, 4, 128, 512)
    dr = drift[0].reshape(8, 2, 4, 64, 512)
    any_spec = pl.BlockSpec(memory_space=pl.ANY)
    vmem_spec = pl.BlockSpec(memory_space=pltpu.VMEM)
    hbm_spec = pl.BlockSpec(memory_space=pltpu.HBM)
    weights, new_outer, new_momentum = pl.pallas_call(
        kernel,
        out_shape=(
            pltpu.VMEM((4, 2, 2, 4, 4, 16, 512), BF16),
            pltpu.VMEM((16, 8192), F32),
            pltpu.VMEM((16, 8192), F32),
        ),
        in_specs=[hbm_spec] * 5,
        out_specs=[any_spec, vmem_spec, vmem_spec],
        scratch_shapes=[
            pltpu.VMEM((128, 4096), BF16),
            pltpu.VMEM((8, 2, 4, 64, 128), BF16),
            pltpu.VMEM((4, 8, 64, 1024), BF16),
            pltpu.VMEM((4, 2, 4, 128, 512), BF16),
            pltpu.VMEM((2, 8, 4, 64, 512), BF16),
            pltpu.VMEM((4, 4, 4, 2, 64, 512), BF16),
            pltpu.VMEM((2, 4, 4, 64, 512), BF16),
            pltpu.VMEM((2, 4, 4, 2, 64, 512), BF16),
            pltpu.VMEM((4, 8, 4, 16, 512), BF16),
            pltpu.VMEM((2, 4, 4, 4, 16, 512), BF16),
            pltpu.VMEM((4, 4, 16, 512), BF16),
            pltpu.VMEM((16, 8192), F32),
            pltpu.VMEM((16, 8192), F32),
            pltpu.VMEM((16, 8192), F32),
            pltpu.VMEM((4, 16, 2048), F32),
            pltpu.VMEM((4, 4, 16, 512), BF16),
            pltpu.VMEM((4, 4, 16, 512), BF16),
            pltpu.SemaphoreType.DMA((POOL + 8,)),
            pltpu.SemaphoreType.DMA((N_RECV,)),
            pltpu.SemaphoreType.DMA((N_LOCAL,)),
        ],
        compiler_params=pltpu.CompilerParams(
            collective_id=0, has_side_effects=True, vmem_limit_bytes=54 * 1024 * 1024
        ),
        name="outer_step",
    )(activations[0], cot, dr, outer_weights, momentum)
    return weights.reshape(4096, 512), new_outer, new_momentum


def solution(mesh):
    in_specs = (
        P("rep", "tp", None),
        P("rep", None, "tp"),
        P("rep", None, "tp"),
        P(("rep", "tp"), None),
        P(("rep", "tp"), None),
    )
    out_specs = (P(None, "tp"), P(("rep", "tp"), None), P(("rep", "tp"), None))
    return jax.shard_map(
        on_device, mesh=mesh, in_specs=in_specs, out_specs=out_specs, check_vma=False
    )
```

time: 488 us -> 133 us (0.27)
  waiting for transfers between devices: 430 us -> 0 us
  Pallas kernels: 0 us -> 128 us
  blocking collectives: 24.2 us -> 0 us
  matrix products: 14.4 us -> 0 us
  between operations: 13.8 us -> 0.64 us
    all_gather x3 -> x0, waiting for transfers between devices: 325 us -> none  [the longest x2 248 us: gathered_by_axis(): nearer = lax.all_gather(shard, axes[-1], axis=dim, tiled=True)]
    pallas_call x0 -> x1, Pallas kernels: none -> 128 us  [on_device(): pl.pallas_call(kernel, out_shape=(pltpu.VMEM((4, 2, 2, 4, 4, 16, 512), BF...]
    reduce_scatter x1 -> x0, waiting for transfers between devices: 104 us -> none  [on_device(): lax.psum_scatter(delta.astype(jnp.float32).astype(jnp.bfloat16), 'rep', s...]
    all_to_all x2 -> x0, blocking collectives: 24.2 us -> none  [the longest x1 12.9 us: on_device(): lax.all_to_all(summed.astype(jnp.bfloat16), TP, split_axis=0, concat_axis...]
    dot_general x1 -> x0, matrix products: 14.4 us -> none  [on_device(): jnp.einsum('td,tf->df', gathered_by_axis(activations, TP, 1)[0], cot_rows...]
  transfers between devices with their start and end apart: 4 -> 0, of which waited for: 4 -> 0; matrix products, arithmetic and copies ran while one was open for 0% -> 0% of each run, Pallas kernels for 0% -> 0%
where the time goes in v3:
time: 133 us; the launch traced here: 132 us
  Pallas kernels  128 us (96%)
  local copies, waits for them, and re-layouts  3.6 us (3%)
    pallas_call x1, Pallas kernels, on_device(): pl.pallas_call(kernel, out_shape=(pltpu.VMEM((4, 2, 2, 4, 4, 16, 512), BF...  128 us
    unnamed x3, local copies, waits for them, and re-layouts  3.6 us

profile of v3, /device:TPU:1, one launch (start us, length us, event | category | flops | bytes accessed | tf_op | source)
XLA Modules:
  0.0 132.4 jit_solution(13527045252161410550)
XLA Ops:
  0.6 128.2 %outer_step.1 = (bf16[4,2,2,4,4,16,512]{6,5,4,3,2,1,0:T(8,128)(2,1)S(1)}, f32[16,8192]{1,0:T(8,128)S(1)}, f32[16,8192]{1,0:T(8,128)S(1)}) custom-call(bf16[128,4096]{1,0:T(8,128)(2,1)} %bitcast.7, bf16[4,4,128,512]{3,2,1,0:T(8,128)(2,1)} %bitcast.6, bf16[8,2,4,64,512]{4,3,2,1,0:T(8,128)(2,1)} %bitcast.5, f32[16,8192]{1,0:T(8,128)} %outer.1, f32[16,8192]{1,0:T(8,128)} %mom.1), custom_call_target="tpu_custom_call" | custom-call | tf_op jit(solution)/shard_map/outer_step/pallas_call | solution.py:444
  128.8 2.0 %copy.11 = bf16[4096,512]{1,0:T(8,128)(2,1)} copy(bf16[4096,512]{1,0:T(8,128)(2,1)S(1)} %bitcast.4) | data formatting | bytes 8388608
  130.8 0.8 copy.12
  131.6 0.8 copy.13

commit v4 on v3

--- a/solution.py
+++ b/solution.py
@@ -422,7 +422,7 @@
         for step in range(steps + 1):
             plan.append((ring + pace * step, ring_z, n, step))
         stop = ring + pace * steps + 0.1
-        begin = max(stop + 4.8, 84.0 + 1.5 * n)
+        begin = max(stop + 4.8, 87.5 + 1.5 * n)
         for when, step in ((stop, update), (begin, gather_own), (begin + 4.4, gather_near),
                            (begin + 8.2, gather_far), (150.0, gather_done)):
             plan.append((when, step, n))

time: 133 us -> 132 us (level)
  no operation moved by 1% of the time
where the time goes in v4:
time: 132 us
  Pallas kernels  128 us (97%)
  local copies, waits for them, and re-layouts  3.6 us (3%)
    pallas_call x1, Pallas kernels, on_device(): pl.pallas_call(kernel, out_shape=(pltpu.VMEM((4, 2, 2, 4, 4, 16, 512), BF...  128 us
    unnamed x3, local copies, waits for them, and re-layouts  3.6 us

profile of v4, /device:TPU:1, one launch (start us, length us, event | category | flops | bytes accessed | tf_op | source)
XLA Modules:
  0.0 132.1 jit_solution(3742254693348776402)
XLA Ops:
  0.6 127.9 %outer_step.1 = (bf16[4,2,2,4,4,16,512]{6,5,4,3,2,1,0:T(8,128)(2,1)S(1)}, f32[16,8192]{1,0:T(8,128)S(1)}, f32[16,8192]{1,0:T(8,128)S(1)}) custom-call(bf16[128,4096]{1,0:T(8,128)(2,1)} %bitcast.7, bf16[4,4,128,512]{3,2,1,0:T(8,128)(2,1)} %bitcast.6, bf16[8,2,4,64,512]{4,3,2,1,0:T(8,128)(2,1)} %bitcast.5, f32[16,8192]{1,0:T(8,128)} %outer.1, f32[16,8192]{1,0:T(8,128)} %mom.1), custom_call_target="tpu_custom_call" | custom-call | tf_op jit(solution)/shard_map/outer_step/pallas_call | solution.py:444
  128.5 2.0 %copy.11 = bf16[4096,512]{1,0:T(8,128)(2,1)} copy(bf16[4096,512]{1,0:T(8,128)(2,1)S(1)} %bitcast.4) | data formatting | bytes 8388608
  130.5 0.8 copy.12
  131.3 0.8 copy.13
